TPU v7x, 32 devices: a whole 2x2x4 slice. The times are simulated.
32 devices in a mesh: dp: 8 (over y, x, core), mp: 4 (over z).
Axes of the slice: x: 2, y: 2, z: 4, core: 2. Of those that a mesh axis runs over, the one named last changes fastest.
Arguments:
- tokens: bfloat16 [8192, 2048], P('dp'), may hold values from -6 to 6
- doc_lengths: int32 [8, 8], P('dp'), may hold values from 1 to 512, 1024 in all within a row
- slot_live: int32 [36], P('mp'), may hold values from 0 to 1, as said below
- attn_gain: bfloat16 [2048], replicated, may hold values from 0.5 to 1.5
- w_query: bfloat16 [2048, 1536], P(None, 'mp'), may hold values from -0.125 to 0.125
- w_keyval: bfloat16 [2048, 768], replicated, may hold values from -0.125 to 0.125
- q_gain: bfloat16 [64], replicated, may hold values from 0.099609375 to 1.8984375
- k_gain: bfloat16 [64], replicated, may hold values from 0.099609375 to 1.8984375
- w_out: bfloat16 [1536, 2048], P('mp'), may hold values from -0.625 to 0.625
- ffn_gain: bfloat16 [2048], replicated, may hold values from 0.5 to 1.5
- w_gate: bfloat16 [2048, 4608], P(None, 'mp'), may hold values from -0.125 to 0.125
- w_up: bfloat16 [2048, 4608], P(None, 'mp'), may hold values from -0.125 to 0.125
- w_down: bfloat16 [4608, 2048], P('mp'), may hold values from -0.09375 to 0.09375
- out_grad: bfloat16 [8192, 2048], P('dp'), may hold values from -6 to 6
Outputs:
- block_out: bfloat16 [8192, 2048], P(('dp', 'mp'))
- grad_tokens: float32 [8192, 2048], P(('dp', 'mp'))
- grad_attn_gain: float32 [2048], replicated
- grad_query: float32 [2048, 1536], P('dp', 'mp')
- grad_keyval: float32 [2048, 768], P(('dp', 'mp'))
- grad_q_gain: float32 [64], replicated
- grad_k_gain: float32 [64], replicated
- grad_out_proj: float32 [1536, 2048], P('mp', 'dp')
- grad_ffn_gain: float32 [2048], replicated
- grad_gate: float32 [2048, 4608], P('dp', 'mp')
- grad_up: float32 [2048, 4608], P('dp', 'mp')
- grad_down: float32 [4608, 2048], P('mp', 'dp')
Inputs may be any that keep to these rules, and one draw needn't show every extreme that they name: `doc_lengths`: each row's 8 lengths sum to 1024, and one of them is 512. `slot_live`: the 9 slots of each index of mp hold 34 // 4 or 34 // 4 + 1 live ones, 34 live in all; which slots and which indices hold more varies.
All inputs are finite; a program needn't handle non-finite values.
Results may differ from a plain program's by a relative error of at most 0.018.
Values may be sent and summed in bfloat16 or wider, within the bound.
A program may use at most 192 MiB of HBM per device.

v0:
```python
import math
import jax
import jax.numpy as jnp
from jax import lax
from jax.sharding import PartitionSpec as P

EPSILON = 1e-06
MASKED = -1000000000.0
ROPE_BASE = 10000.0
HIGHEST_PREC = lax.Precision.HIGHEST
CONTRACT_LAST = (((1,), (1,)), ((), ()))
CONTRACT_FIRST = (((0,), (0,)), ((), ()))


def normalize(raw_in):
    return raw_in * lax.rsqrt(jnp.mean(raw_in * raw_in, axis=-1, keepdims=True) + EPSILON)


def norm_back(grad_normed, raw_in, gain_vec):
    factor = lax.rsqrt(jnp.mean(raw_in * raw_in, axis=-1, keepdims=True) + EPSILON)
    unit_rows = raw_in * factor
    scaled = grad_normed * gain_vec
    grad_raw = factor * (scaled - unit_rows * jnp.mean(scaled * unit_rows, axis=-1, keepdims=True))
    return (grad_raw, jnp.sum(grad_normed * unit_rows, axis=tuple(range(raw_in.ndim - 1))))


def rotate(values, cosine_tab, sine_tab, sign):
    half_size = values.shape[-1] // 2
    first_half = values[..., :half_size]
    second_half = values[..., half_size:]
    return jnp.concatenate(
        [
            first_half * cosine_tab - sign * second_half * sine_tab,
            second_half * cosine_tab + sign * first_half * sine_tab,
        ],
        axis=-1,
    )


def doc_layout(lengths, row_count):
    doc_ends = jnp.cumsum(lengths)
    token_index = jnp.arange(row_count, dtype=jnp.int32)
    past_end = (token_index[:, None] >= doc_ends[None, :]).astype(jnp.int32)
    doc_id = jnp.sum(past_end, axis=1)
    doc_pos = token_index - jnp.sum(past_end * lengths[None, :], axis=1)
    return (doc_id, doc_pos, token_index)


def rope_table(doc_pos, head_size):
    rope_freq = jnp.exp(
        jnp.arange(head_size // 2, dtype=jnp.float32) * (-2.0 * math.log(ROPE_BASE) / head_size)
    )
    rope_angle = doc_pos.astype(jnp.float32)[:, None] * rope_freq[None, :]
    return (jnp.cos(rope_angle)[:, None, :], jnp.sin(rope_angle)[:, None, :])


def shards(
    tokens,
    doc_lengths,
    slot_live,
    attn_gain,
    w_query,
    w_keyval,
    q_gain,
    k_gain,
    w_out,
    ffn_gain,
    w_gate,
    w_up,
    w_down,
    out_grad,
):
    row_count, model_width = tokens.shape
    head_size = q_gain.shape[0]
    heads_dev = w_query.shape[1] // head_size
    heads_all = heads_dev * lax.axis_size("mp")
    kv_heads = w_keyval.shape[1] // (2 * head_size)
    group_size = heads_all // kv_heads
    kv_window = min(kv_heads, (heads_dev + group_size - 2) // group_size + 1)
    tile_cols = w_gate.shape[1] // slot_live.shape[0]
    shard_rows = row_count // lax.axis_size("mp")
    block_rows = min(512, row_count)
    score_scale = head_size ** (-0.5)
    head_span = heads_dev * head_size
    mp_index = lax.axis_index("mp")
    row_first = mp_index * shard_rows
    q_first = mp_index * heads_dev
    kv_first = jnp.minimum(q_first // group_size, kv_heads - kv_window)
    kv_owner = (q_first + jnp.arange(heads_dev, dtype=jnp.int32)) // group_size - kv_first
    head_pick = (kv_owner[:, None] == jnp.arange(kv_window, dtype=jnp.int32)[None, :]).astype(
        jnp.float32
    )
    key_cols = lax.dynamic_slice_in_dim(w_keyval, kv_first * head_size, kv_window * head_size, 1)
    value_cols = lax.dynamic_slice_in_dim(
        w_keyval, (kv_heads + kv_first) * head_size, kv_window * head_size, 1
    )

    def spread(window_cols):
        return (
            jnp.einsum(
                "dwe,hw->dhe",
                window_cols.reshape(model_width, kv_window, head_size),
                head_pick.astype(jnp.bfloat16),
                preferred_element_type=jnp.float32,
            )
            .astype(jnp.bfloat16)
            .reshape(model_width, head_span)
        )

    def fold_heads(per_head):
        return jnp.einsum(
            "dhe,hw->dwe",
            per_head.reshape(model_width, heads_dev, head_size),
            head_pick,
            precision=HIGHEST_PREC,
        ).reshape(model_width, kv_window * head_size)

    doc_id, doc_pos, token_index = doc_layout(doc_lengths[0], row_count)
    cosine_tab, sine_tab = rope_table(doc_pos, head_size)
    x_float = tokens.astype(jnp.float32)
    x_rows = lax.dynamic_slice_in_dim(x_float, row_first, shard_rows, 0)
    gain_one = attn_gain.astype(jnp.float32)
    gain_two = ffn_gain.astype(jnp.float32)
    q_gain_f = q_gain.astype(jnp.float32)
    k_gain_f = k_gain.astype(jnp.float32)
    xn_one = (normalize(x_float) * gain_one).astype(jnp.bfloat16)
    q_raw = jnp.dot(xn_one, w_query, preferred_element_type=jnp.float32).reshape(
        row_count, heads_dev, head_size
    )
    kv_raw = jnp.dot(
        xn_one, jnp.concatenate([key_cols, value_cols], axis=1), preferred_element_type=jnp.float32
    ).reshape(row_count, 2, kv_window, head_size)
    k_raw = jnp.einsum("twe,hw->the", kv_raw[:, 0], head_pick, precision=HIGHEST_PREC)
    v_raw = jnp.einsum("twe,hw->the", kv_raw[:, 1], head_pick, precision=HIGHEST_PREC)
    q_rot = rotate(normalize(q_raw) * q_gain_f, cosine_tab, sine_tab, 1.0).astype(jnp.bfloat16)
    k_rot = rotate(normalize(k_raw) * k_gain_f, cosine_tab, sine_tab, 1.0).astype(jnp.bfloat16)
    v_low = v_raw.astype(jnp.bfloat16)

    def block_scores(row_start, key_stop):
        scores = (
            jnp.einsum(
                "qhe,khe->hqk",
                q_rot[row_start : row_start + block_rows],
                k_rot[:key_stop],
                preferred_element_type=jnp.float32,
            )
            * score_scale
        )
        allowed = (doc_id[row_start : row_start + block_rows, None] == doc_id[None, :key_stop]) & (
            token_index[None, :key_stop] <= token_index[row_start : row_start + block_rows, None]
        )
        return jnp.where(allowed[None], scores, MASKED)

    block_outs = []
    block_lse = []
    for row_start in range(0, row_count, block_rows):
        key_stop = row_start + block_rows
        scores = block_scores(row_start, key_stop)
        row_max = jnp.max(scores, axis=-1, keepdims=True)
        shifted = jnp.exp(scores - row_max)
        row_total = jnp.sum(shifted, axis=-1, keepdims=True)
        attn_probs = (shifted / row_total).astype(jnp.bfloat16)
        block_outs.append(
            jnp.einsum(
                "hqk,khe->qhe", attn_probs, v_low[:key_stop], preferred_element_type=jnp.float32
            )
        )
        block_lse.append(row_max + jnp.log(row_total))
    attended = (
        jnp.concatenate(block_outs, axis=0).reshape(row_count, head_span).astype(jnp.bfloat16)
    )
    attn_part = jnp.dot(attended, w_out, preferred_element_type=jnp.float32)
    hidden_full = x_float + lax.psum(attn_part, "mp")
    hidden_rows = lax.dynamic_slice_in_dim(hidden_full, row_first, shard_rows, 0)
    xn_two = (normalize(hidden_full) * gain_two).astype(jnp.bfloat16)
    live_cols = jnp.repeat(slot_live.astype(jnp.float32), tile_cols)
    gate_act = jnp.dot(xn_two, w_gate, preferred_element_type=jnp.float32)
    up_act = jnp.dot(xn_two, w_up, preferred_element_type=jnp.float32)
    gate_sigmoid = jax.nn.sigmoid(gate_act)
    gate_silu = gate_act * gate_sigmoid
    ffn_hidden = (gate_silu * up_act * live_cols).astype(jnp.bfloat16)
    ffn_part = jnp.dot(ffn_hidden, w_down, preferred_element_type=jnp.float32)
    out_rows = hidden_rows + lax.psum_scatter(
        ffn_part.astype(jnp.bfloat16), "mp", scatter_dimension=0, tiled=True
    ).astype(jnp.float32)
    block_out = out_rows.astype(jnp.bfloat16)
    d_hidden = (
        lax.dot_general(out_grad, w_down, CONTRACT_LAST, preferred_element_type=jnp.float32)
        * live_cols
    )
    grad_down = lax.dot_general(
        ffn_hidden, out_grad, CONTRACT_FIRST, preferred_element_type=jnp.float32
    )
    d_gate = (d_hidden * up_act * gate_sigmoid * (1.0 + gate_act * (1.0 - gate_sigmoid))).astype(
        jnp.bfloat16
    )
    d_up = (d_hidden * gate_silu).astype(jnp.bfloat16)
    grad_gate = lax.dot_general(xn_two, d_gate, CONTRACT_FIRST, preferred_element_type=jnp.float32)
    grad_up = lax.dot_general(xn_two, d_up, CONTRACT_FIRST, preferred_element_type=jnp.float32)
    dn_two_part = lax.dot_general(
        d_gate, w_gate, CONTRACT_LAST, preferred_element_type=jnp.float32
    ) + lax.dot_general(d_up, w_up, CONTRACT_LAST, preferred_element_type=jnp.float32)
    dn_two = lax.psum(dn_two_part, "mp")
    back_two, _ = norm_back(dn_two, hidden_full, gain_two)
    dh_full = out_grad.astype(jnp.float32) + back_two
    dh_rows = lax.dynamic_slice_in_dim(dh_full, row_first, shard_rows, 0)
    grad_gain_two = jnp.sum(
        lax.dynamic_slice_in_dim(dn_two, row_first, shard_rows, 0) * normalize(hidden_rows), axis=0
    )
    dh_low = dh_full.astype(jnp.bfloat16)
    grad_out_proj = lax.dot_general(
        attended, dh_low, CONTRACT_FIRST, preferred_element_type=jnp.float32
    )
    d_att = lax.dot_general(dh_low, w_out, CONTRACT_LAST, preferred_element_type=jnp.float32)
    d_att = d_att.astype(jnp.bfloat16).reshape(row_count, heads_dev, head_size)
    dq_blocks = []
    d_keys = jnp.zeros((row_count, heads_dev, head_size), jnp.float32)
    d_values = jnp.zeros((row_count, heads_dev, head_size), jnp.float32)
    for block_index, row_start in enumerate(range(0, row_count, block_rows)):
        key_stop = row_start + block_rows
        scores = block_scores(row_start, key_stop)
        attn_probs = jnp.exp(scores - block_lse[block_index])
        probs_low = attn_probs.astype(jnp.bfloat16)
        att_rows = d_att[row_start:key_stop]
        d_probs = jnp.einsum(
            "qhe,khe->hqk", att_rows, v_low[:key_stop], preferred_element_type=jnp.float32
        )
        d_scores = (
            attn_probs * (d_probs - jnp.sum(d_probs * attn_probs, axis=-1, keepdims=True))
        ).astype(jnp.bfloat16)
        dq_blocks.append(
            jnp.einsum(
                "hqk,khe->qhe", d_scores, k_rot[:key_stop], preferred_element_type=jnp.float32
            )
            * score_scale
        )
        d_keys = d_keys.at[:key_stop].add(
            jnp.einsum(
                "hqk,qhe->khe",
                d_scores,
                q_rot[row_start:key_stop],
                preferred_element_type=jnp.float32,
            )
            * score_scale
        )
        d_values = d_values.at[:key_stop].add(
            jnp.einsum("hqk,qhe->khe", probs_low, att_rows, preferred_element_type=jnp.float32)
        )
    d_queries = jnp.concatenate(dq_blocks, axis=0)
    dq_raw, grad_q_gain = norm_back(rotate(d_queries, cosine_tab, sine_tab, -1.0), q_raw, q_gain_f)
    dk_raw, grad_k_gain = norm_back(rotate(d_keys, cosine_tab, sine_tab, -1.0), k_raw, k_gain_f)
    d_proj = jnp.concatenate(
        [
            dq_raw.reshape(row_count, head_span),
            dk_raw.reshape(row_count, head_span),
            d_values.reshape(row_count, head_span),
        ],
        axis=1,
    ).astype(jnp.bfloat16)
    w_proj = jnp.concatenate([w_query, spread(key_cols), spread(value_cols)], axis=1)
    dn_one_part = lax.dot_general(d_proj, w_proj, CONTRACT_LAST, preferred_element_type=jnp.float32)
    grad_proj = lax.dot_general(xn_one, d_proj, CONTRACT_FIRST, preferred_element_type=jnp.float32)
    grad_query = grad_proj[:, :head_span]
    grad_keyval = jnp.zeros((model_width, 2 * kv_heads * head_size), jnp.float32)
    grad_keyval = lax.dynamic_update_slice_in_dim(
        grad_keyval, fold_heads(grad_proj[:, head_span : 2 * head_span]), kv_first * head_size, 1
    )
    grad_keyval = lax.dynamic_update_slice_in_dim(
        grad_keyval, fold_heads(grad_proj[:, 2 * head_span :]), (kv_heads + kv_first) * head_size, 1
    )
    dn_one_rows = lax.psum_scatter(
        dn_one_part.astype(jnp.bfloat16), "mp", scatter_dimension=0, tiled=True
    ).astype(jnp.float32)
    back_one, grad_gain_one = norm_back(dn_one_rows, x_rows, gain_one)
    grad_tokens = dh_rows + back_one
    grad_query, grad_out_proj, grad_gate, grad_up, grad_down = (
        lax.psum_scatter(
            grad_query.astype(jnp.bfloat16), "dp", scatter_dimension=0, tiled=True
        ).astype(jnp.float32),
        lax.psum_scatter(
            grad_out_proj.astype(jnp.bfloat16), "dp", scatter_dimension=1, tiled=True
        ).astype(jnp.float32),
        lax.psum_scatter(
            grad_gate.astype(jnp.bfloat16), "dp", scatter_dimension=0, tiled=True
        ).astype(jnp.float32),
        lax.psum_scatter(
            grad_up.astype(jnp.bfloat16), "dp", scatter_dimension=0, tiled=True
        ).astype(jnp.float32),
        lax.psum_scatter(
            grad_down.astype(jnp.bfloat16), "dp", scatter_dimension=1, tiled=True
        ).astype(jnp.float32),
    )
    grad_keyval = lax.psum_scatter(grad_keyval, ("dp", "mp"), scatter_dimension=0, tiled=True)
    grad_gain_one, grad_gain_two, grad_q_gain, grad_k_gain = lax.psum(
        (grad_gain_one, grad_gain_two, grad_q_gain, grad_k_gain), ("dp", "mp")
    )
    return (
        block_out,
        grad_tokens,
        grad_gain_one,
        grad_query,
        grad_keyval,
        grad_q_gain,
        grad_k_gain,
        grad_out_proj,
        grad_gain_two,
        grad_gate,
        grad_up,
        grad_down,
    )


def solution(mesh):
    return jax.shard_map(
        shards,
        mesh=mesh,
        in_specs=(
            P("dp", None),
            P("dp", None),
            P("mp"),
            P(),
            P(None, "mp"),
            P(),
            P(),
            P(),
            P("mp", None),
            P(),
            P(None, "mp"),
            P(None, "mp"),
            P("mp", None),
            P("dp", None),
        ),
        out_specs=(
            P(("dp", "mp"), None),
            P(("dp", "mp"), None),
            P(),
            P("dp", "mp"),
            P(("dp", "mp"), None),
            P(),
            P(),
            P("mp", "dp"),
            P(),
            P("dp", "mp"),
            P("dp", "mp"),
            P("mp", "dp"),
        ),
        check_vma=False,
    )
```

profile of v0, /device:TPU:0, one launch (start us, length us, event | category | flops | bytes accessed | tf_op | source)
XLA Modules:
  0.0 1244.2 jit_solution(17080760547115743847)
XLA Ops:
  63.2 292.8 %all-reduce.6.cloned.1.call-done = f32[1024,2048]{1,0:T(8,128)} async-done(((f32[1024,2048]{1,0:T(8,128)}), f32[1024,2048]{1,0:T(8,128)}) %all-reduce.6.cloned.1.call-update) | async-done | bytes 8388624 | tf_op jit(solution)/shard_map/psum | solution.py:173
  364.9 11.4 fusion.111
  376.4 7.3 fusion.112
  383.7 12.7 %multiply_convert_fusion.4 = (bf16[1024,1152]{1,0:T(8,128)(2,1)S(1)}, bf16[1024,1152]{1,0:T(8,128)(2,1)}, bf16[1024,1152]{1,0:T(8,128)(2,1)}) fusion(f32[1024,1152]{1,0:T(8,128)} %fusion.111, f32[1024,1152]{1,0:T(8,128)} %fusion.112, f32[1152]{0:T(1024)S(1)} %broadcast_bitcast_fusion, bf16[1024,2048]{1,0:T(8,128)(2,1)S(1)} %copy-done.27, ...), kind=kOutput, calls=%fused_computation.36 | convolution fusion | flops 4851892224 | bytes 25432576 | tf_op jit(solution)/shard_map/dot_general | solution.py:188
  396.5 8.1 fusion.113
  404.6 8.5 convolution_add_fusion
  413.3 9.6 convolution_convert_fusion.2
  422.9 9.6 convolution_convert_fusion.1
  432.6 9.2 convolution_convert_fusion
  442.5 9.5 convolution_convert_fusion.3
  452.1 251.1 %all-reduce.8.cloned.1.call-done = f32[1024,2048]{1,0:T(8,128)} async-done(((f32[1024,2048]{1,0:T(8,128)}), f32[1024,2048]{1,0:T(8,128)}) %all-reduce.8.cloned.1.call-update) | async-done | bytes 8388624 | tf_op jit(solution)/shard_map/psum | solution.py:203
  703.2 6.9 multiply_reduce_fusion.1
  713.0 8.3 multiply_add_fusion
  748.9 6.9 multiply_convert_fusion
  792.5 7.4 fusion.19
  823.2 11.5 dynamic_update_slice.6
  834.7 11.0 dynamic_update_slice.7
  860.3 13.2 %reduce-scatter.23.cloned.1.call-done = bf16[1152,256]{1,0:T(8,128)(2,1)} async-done(((bf16[1152,2048]{1,0:T(8,128)(2,1)}), bf16[1152,256]{1,0:T(8,128)(2,1)}) %reduce-scatter.23.cloned.1.call-update) | async-done | bytes 589840 | tf_op jit(solution)/shard_map/reduce_scatter | solution.py:289
  875.8 76.7 %reduce-scatter.9.cloned.1.call-done = bf16[256,2048]{1,0:T(8,128)(2,1)} async-done(((bf16[1024,2048]{1,0:T(8,128)(2,1)}), bf16[256,2048]{1,0:T(8,128)(2,1)}) %reduce-scatter.9.cloned.1.call-update) | async-done | bytes 1048592 | tf_op jit(solution)/shard_map/reduce_scatter | solution.py:183
  956.6 38.2 %reduce-scatter.13.cloned.1.call-done = bf16[256,384]{0,1:T(8,128)(2,1)} async-done(((bf16[2048,384]{0,1:T(8,128)(2,1)}), bf16[256,384]{0,1:T(8,128)(2,1)}) %reduce-scatter.13.cloned.1.call-update) | async-done | bytes 196624 | tf_op jit(solution)/shard_map/reduce_scatter | solution.py:277
  996.5 39.9 %reduce-scatter.17.cloned.1.call-done = bf16[384,256]{1,0:T(8,128)(2,1)} async-done(((bf16[384,2048]{1,0:T(8,128)(2,1)}), bf16[384,256]{1,0:T(8,128)(2,1)}) %reduce-scatter.17.cloned.1.call-update) | async-done | bytes 196624 | tf_op jit(solution)/shard_map/reduce_scatter | solution.py:280
  1038.1 77.4 %reduce-scatter.11.cloned.1.call-done = bf16[256,2048]{1,0:T(8,128)(2,1)} async-done(((bf16[1024,2048]{1,0:T(8,128)(2,1)}), bf16[256,2048]{1,0:T(8,128)(2,1)}) %reduce-scatter.11.cloned.1.call-update) | async-done | bytes 1048592 | tf_op jit(solution)/shard_map/reduce_scatter | solution.py:271
  1118.2 41.1 %all-reduce.2 = (f32[2048]{0:T(1024)}, f32[64]{0:T(128)}, f32[64]{0:T(128)}, f32[2048]{0:T(1024)}) all-reduce(f32[2048]{0:T(1024)S(1)} %get-tuple-element.124, f32[64]{0:T(128)S(1)} %reduce_sum.217, f32[64]{0:T(128)S(1)} %get-tuple-element.126, f32[2048]{0:T(1024)S(1)} %get-tuple-element.141), channel_id=1, replica_groups=mesh['dp'=8,'mp'=4] {'dp','mp'}, use_global_device_ids=true, to_apply=%region_23.24 | all-reduce | flops 4224 | bytes 33792 | tf_op jit(solution)/shard_map/psum | solution.py:294
  1163.9 73.2 %reduce-scatter.15.cloned.1.call-done = f32[64,768]{1,0:T(8,128)} async-done(((f32[2048,768]{1,0:T(8,128)}), f32[64,768]{1,0:T(8,128)}) %reduce-scatter.15.cloned.1.call-update) | async-done | bytes 196624 | tf_op jit(solution)/shard_map/reduce_scatter | solution.py:293
  (289 shorter events, 187.0 us)
Async XLA Ops:
  7.2 49.6 %copy-start = (bf16[384,2048]{1,0:T(8,128)(2,1)S(1)}, bf16[384,2048]{1,0:T(8,128)(2,1)}, u32[]{:S(2)}) copy-start(bf16[384,2048]{1,0:T(8,128)(2,1)} %param.34) | copy-start | bytes 4718596
  7.2 348.8 %all-reduce.6.cloned.1.call-start = ((), (), s32[]{:S(2)}) async-start(), calls=%async_computation.8 | async-start | bytes 16777216 | tf_op jit(solution)/shard_map/psum | solution.py:173
  7.3 27.2 %copy-start.54 = (s32[6]{0:T(128)}, s32[6]{0:T(128)S(1)}, u32[]{:S(2)}) copy-start(s32[6]{0:T(128)S(1)} %fusion.88) | copy-start | bytes 76
  8.2 16.5 %copy-start.52 = (f32[2048]{0:T(1024)}, f32[2048]{0:T(1024)S(1)}, u32[]{:S(2)}) copy-start(f32[2048]{0:T(1024)S(1)} %convert_element_type.146) | copy-start | bytes 24580
  11.6 27.6 %copy-start.61 = (f32[64]{0:T(128)}, f32[64]{0:T(128)S(1)}, u32[]{:S(2)}) copy-start(f32[64]{0:T(128)S(1)} %convert_element_type.151) | copy-start | bytes 772
  15.1 24.2 %copy-start.10 = (f32[1024,384]{0,1:T(8,128)}, f32[1024,384]{0,1:T(8,128)S(1)}, u32[]{:S(2)}) copy-start(f32[1024,384]{0,1:T(8,128)S(1)} %fusion.103) | copy-start | bytes 4718596
  15.3 23.9 %copy-start.45 = (f32[1024,6]{0,1:T(8,128)}, f32[1024,6]{0,1:T(8,128)S(1)}, u32[]{:S(2)}) copy-start(f32[1024,6]{0,1:T(8,128)S(1)} %add_rsqrt_fusion.1) | copy-start | bytes 73732
  15.3 23.9 %copy-start.56 = (f32[64]{0:T(128)}, f32[64]{0:T(128)S(1)}, u32[]{:S(2)}) copy-start(f32[64]{0:T(128)S(1)} %convert_element_type.153) | copy-start | bytes 772
  37.4 16.6 %copy-start.36 = (bf16[512,6,64]{0,1,2:T(8,128)(2,1)}, bf16[512,6,64]{0,1,2:T(8,128)(2,1)S(1)}, u32[]{:S(2)}) copy-start(bf16[512,6,64]{0,1,2:T(8,128)(2,1)S(1)} %slice.197) | copy-start | bytes 1179652
  62.5 640.7 %all-reduce.8.cloned.1.call-start = ((), (), s32[]{:S(2)}) async-start(), calls=%async_computation.10 | async-start | bytes 16777216 | tf_op jit(solution)/shard_map/psum | solution.py:203
  361.7 14.6 %slice-start.7 = ((s8[4718592]{0:T(1024)(128)(4,1)}), s8[524288]{0:T(1024)(128)(4,1)S(1)}, s32[]{:S(2)}) async-start(s8[4718592]{0:T(1024)(128)(4,1)} %bitcast.161), calls=%async_computation.25 | async-start | bytes 1048576
  376.4 20.1 %slice-start.5 = ((s8[4718592]{0:T(1024)(128)(4,1)}), s8[4194304]{0:T(1024)(128)(4,1)S(1)}, s32[]{:S(2)}) async-start(s8[4718592]{0:T(1024)(128)(4,1)} %bitcast.159), calls=%async_computation.23 | async-start | bytes 8388608
  376.4 28.3 %slice-start.9 = ((s8[4718592]{0:T(1024)(128)(4,1)}), s8[4194304]{0:T(1024)(128)(4,1)S(1)}, s32[]{:S(2)}) async-start(s8[4718592]{0:T(1024)(128)(4,1)} %bitcast.163), calls=%async_computation.27 | async-start | bytes 8388608
  383.7 20.9 %slice-start.10 = ((s8[4718592]{0:T(1024)(128)(4,1)}), s8[524288]{0:T(1024)(128)(4,1)S(1)}, s32[]{:S(2)}) async-start(s8[4718592]{0:T(1024)(128)(4,1)} %bitcast.163), calls=%async_computation.28 | async-start | bytes 1048576
  413.2 442.8 %reduce-scatter.19.cloned.1.call-start = ((), (), s32[]{:S(2)}) async-start(), calls=%async_computation.15 | async-start | bytes 5308416 | tf_op jit(solution)/shard_map/reduce_scatter | solution.py:283
  422.9 435.3 %reduce-scatter.21.cloned.1.call-start = ((), (), s32[]{:S(2)}) async-start(), calls=%async_computation.16 | async-start | bytes 5308416 | tf_op jit(solution)/shard_map/reduce_scatter | solution.py:286
  432.5 441.0 %reduce-scatter.23.cloned.1.call-start = ((), (), s32[]{:S(2)}) async-start(), calls=%async_computation.17 | async-start | bytes 5308416 | tf_op jit(solution)/shard_map/reduce_scatter | solution.py:289
  441.8 510.8 %reduce-scatter.9.cloned.1.call-start = ((), (), s32[]{:S(2)}) async-start(), calls=%async_computation.9 | async-start | bytes 5242880 | tf_op jit(solution)/shard_map/reduce_scatter | solution.py:183
  442.5 284.9 %copy-start.50 = (f32[6,512]{1,0:T(8,128)}, f32[6,512]{1,0:T(8,128)S(1)}, u32[]{:S(2)}) copy-start(f32[6,512]{1,0:T(8,128)S(1)} %log_add_fusion.1) | copy-start | bytes 36868
  452.0 542.7 %reduce-scatter.13.cloned.1.call-start = ((), (), s32[]{:S(2)}) async-start(), calls=%async_computation.12 | async-start | bytes 1769472 | tf_op jit(solution)/shard_map/reduce_scatter | solution.py:277
  710.1 17.3 %slice-start.3 = ((s8[6291456]{0:T(1024)(128)(4,1)}), s8[4194304]{0:T(1024)(128)(4,1)S(1)}, s32[]{:S(2)}) async-start(s8[6291456]{0:T(1024)(128)(4,1)} %bitcast.132), calls=%async_computation.21 | async-start | bytes 8388608
  779.3 257.2 %reduce-scatter.17.cloned.1.call-start = ((), (), s32[]{:S(2)}) async-start(), calls=%async_computation.14 | async-start | bytes 1769472 | tf_op jit(solution)/shard_map/reduce_scatter | solution.py:280
  785.7 329.8 %reduce-scatter.11.cloned.1.call-start = ((), (), s32[]{:S(2)}) async-start(), calls=%async_computation.11 | async-start | bytes 5242880 | tf_op jit(solution)/shard_map/reduce_scatter | solution.py:271
  799.9 437.2 %reduce-scatter.15.cloned.1.call-start = ((), (), s32[]{:S(2)}) async-start(), calls=%async_computation.13 | async-start | bytes 6488064 | tf_op jit(solution)/shard_map/reduce_scatter | solution.py:293
  (66 other events, 325.0 us)
Sparse Core Ops, SparseCore 0:
  62.6 293.3 all-reduce.5
  413.3 289.8 all-reduce.7
  706.6 52.7 reduce-scatter.18
  762.7 53.7 reduce-scatter.20
  819.9 53.6 reduce-scatter.22
  875.7 76.7 reduce-scatter.8
  955.8 38.8 reduce-scatter.12
  998.0 38.3 reduce-scatter.16
  1038.7 76.7 reduce-scatter.10
  1121.6 115.4 reduce-scatter.14
where the time goes:
time: 1250 us; the launch traced here: 1240 us
  waiting for transfers between devices  863 us (69%)
  matrix products  172 us (14%)
  other arithmetic  80.4 us (6%)
  local copies, waits for them, and re-layouts  71.4 us (6%)
  blocking collectives  41.1 us (3%)
  between operations  15.7 us (1%)
    psum x1, waiting for transfers between devices, shards(): hidden_full = x_float + lax.psum(attn_part, 'mp')  293 us
    psum x1, waiting for transfers between devices, shards(): dn_two = lax.psum(dn_two_part, 'mp')  251 us
    reduce_scatter x1, waiting for transfers between devices, shards(): lax.psum_scatter(dn_one_part.astype(jnp.bfloat16), 'mp', scatter_dimensio...  77.4 us
    reduce_scatter x1, waiting for transfers between devices, shards(): lax.psum_scatter(ffn_part.astype(jnp.bfloat16), 'mp', scatter_dimension=0...  76.7 us
    reduce_scatter x1, waiting for transfers between devices, shards(): lax.psum_scatter(grad_keyval, ('dp', 'mp'), scatter_dimension=0, tiled=True)  73.2 us
    psum x1, blocking collectives, shards(): lax.psum((grad_gain_one, grad_gain_two, grad_q_gain, grad_k_gain), ('dp',...  41.1 us
    reduce_scatter x1, waiting for transfers between devices, shards(): lax.psum_scatter(grad_out_proj.astype(jnp.bfloat16), 'dp', scatter_dimens...  39.9 us
    reduce_scatter x1, waiting for transfers between devices, shards(): lax.psum_scatter(grad_query.astype(jnp.bfloat16), 'dp', scatter_dimension...  38.2 us
  transfers between devices with their start and end apart: 10, of which 8 were waited for; matrix products, arithmetic and copies ran while one was open for 16% of the time, Pallas kernels for 0%

commit v1 on v0

--- a/solution.py
+++ b/solution.py
@@ -200,7 +200,9 @@
     dn_two_part = lax.dot_general(
         d_gate, w_gate, CONTRACT_LAST, preferred_element_type=jnp.float32
     ) + lax.dot_general(d_up, w_up, CONTRACT_LAST, preferred_element_type=jnp.float32)
-    dn_two = lax.psum(dn_two_part, "mp")
+    dn_two = dn_two_part
+    for hop in (1, 2):
+        dn_two = dn_two + lax.ppermute(dn_two, "mp", [(dev, dev ^ hop) for dev in range(4)])
     back_two, _ = norm_back(dn_two, hidden_full, gain_two)
     dh_full = out_grad.astype(jnp.float32) + back_two
     dh_rows = lax.dynamic_slice_in_dim(dh_full, row_first, shard_rows, 0)

time: 1250 us -> 1410 us (1.13)
  waiting for transfers between devices: 863 us -> 1020 us
  other arithmetic: 80.4 us -> 96.7 us
    ppermute x0 -> x2, waiting for transfers between devices: none -> 584 us  [shards(): lax.ppermute(dn_two, 'mp', [(dev, dev ^ hop) for dev in range(4)])]
    psum x1 -> x0, waiting for transfers between devices: 251 us -> none  [shards(): dn_two = lax.psum(dn_two_part, 'mp')]
    reduce_scatter x1, waiting for transfers between devices: 76.7 us -> 0.01 us  [shards(): lax.psum_scatter(ffn_part.astype(jnp.bfloat16), 'mp', scatter_dimension=0...]
    reduce_scatter x1, waiting for transfers between devices: 39.9 us -> 0.01 us  [shards(): lax.psum_scatter(grad_out_proj.astype(jnp.bfloat16), 'dp', scatter_dimens...]
    reduce_scatter x1, waiting for transfers between devices: 38.2 us -> 0.01 us  [shards(): lax.psum_scatter(grad_query.astype(jnp.bfloat16), 'dp', scatter_dimension...]
  transfers between devices with their start and end apart: 10 -> 11, of which waited for: 8 -> 5; matrix products, arithmetic and copies ran while one was open for 16% -> 16% of each run, Pallas kernels for 0% -> 0%
where the time goes in v1:
time: 1410 us
  waiting for transfers between devices  1020 us (72%)
  matrix products  166 us (12%)
  other arithmetic  96.7 us (7%)
  local copies, waits for them, and re-layouts  69.7 us (5%)
  blocking collectives  41.2 us (3%)
  between operations  15.4 us (1%)
    ppermute x2, waiting for transfers between devices, shards(): lax.ppermute(dn_two, 'mp', [(dev, dev ^ hop) for dev in range(4)])  584 us
    psum x1, waiting for transfers between devices, shards(): hidden_full = x_float + lax.psum(attn_part, 'mp')  293 us
    reduce_scatter x1, waiting for transfers between devices, shards(): lax.psum_scatter(grad_keyval, ('dp', 'mp'), scatter_dimension=0, tiled=True)  73.3 us
    reduce_scatter x1, waiting for transfers between devices, shards(): lax.psum_scatter(dn_one_part.astype(jnp.bfloat16), 'mp', scatter_dimensio...  68.3 us
    psum x1, blocking collectives, shards(): lax.psum((grad_gain_one, grad_gain_two, grad_q_gain, grad_k_gain), ('dp',...  41.2 us
  transfers between devices with their start and end apart: 11, of which 5 were waited for; matrix products, arithmetic and copies ran while one was open for 16% of the time, Pallas kernels for 0%

profile of v1, /device:TPU:0, one launch (start us, length us, event | category | flops | bytes accessed | tf_op | source)
XLA Modules:
  0.0 1409.6 jit_solution(16432284653603223637)
XLA Ops:
  62.9 292.8 %all-reduce.5.cloned.1.call-done = f32[1024,2048]{1,0:T(8,128)} async-done(((f32[1024,2048]{1,0:T(8,128)}), f32[1024,2048]{1,0:T(8,128)}) %all-reduce.5.cloned.1.call-update) | async-done | bytes 8388624 | tf_op jit(solution)/shard_map/psum | solution.py:173
  364.7 11.7 fusion.111
  376.4 7.3 fusion.112
  383.7 12.1 multiply_convert_fusion.4
  397.2 7.4 convolution_convert_fusion.2
  404.6 8.5 fusion.113
  413.2 10.9 convolution_add_fusion
  424.0 7.3 convolution_convert_fusion.1
  431.4 175.0 %collective-permute-done = f32[1024,2048]{1,0:T(8,128)} collective-permute-done((f32[1024,2048]{1,0:T(8,128)}, f32[1024,2048]{1,0:T(8,128)}, u32[]{:S(2)}, u32[]{:S(2)}) %collective-permute-start) | collective-permute-done | bytes 8388640 | tf_op jit(solution)/shard_map/ppermute | solution.py:205
  606.4 11.8 add.217
  619.6 8.5 convolution_convert_fusion
  628.9 9.7 convolution_convert_fusion.3
  638.7 409.1 %collective-permute-done.1 = f32[1024,2048]{1,0:T(8,128)} collective-permute-done((f32[1024,2048]{1,0:T(8,128)}, f32[1024,2048]{1,0:T(8,128)}, u32[]{:S(2)}, u32[]{:S(2)}) %collective-permute-start.1) | collective-permute-done | bytes 8388640 | tf_op jit(solution)/shard_map/ppermute | solution.py:205
  1047.8 12.7 multiply_reduce_fusion.1
  1060.5 7.1 multiply_add_fusion
  1092.4 6.7 multiply_convert_fusion
  1122.4 6.4 convolution_convert_fusion.6
  1135.5 7.4 fusion.19
  1166.2 11.2 dynamic_update_slice.6
  1177.4 11.0 dynamic_update_slice.7
  1188.4 6.6 convert_element_type.145
  1212.9 68.3 %reduce-scatter.11.cloned.1.call-done = bf16[256,2048]{1,0:T(8,128)(2,1)} async-done(((bf16[1024,2048]{1,0:T(8,128)(2,1)}), bf16[256,2048]{1,0:T(8,128)(2,1)}) %reduce-scatter.11.cloned.1.call-update) | async-done | bytes 1048592 | tf_op jit(solution)/shard_map/reduce_scatter | solution.py:273
  1283.8 41.2 %all-reduce.2 = (f32[2048]{0:T(1024)}, f32[64]{0:T(128)}, f32[64]{0:T(128)}, f32[2048]{0:T(1024)}) all-reduce(f32[2048]{0:T(1024)S(1)} %get-tuple-element.124, f32[64]{0:T(128)S(1)} %reduce_sum.217, f32[64]{0:T(128)S(1)} %get-tuple-element.126, f32[2048]{0:T(1024)S(1)} %get-tuple-element.143), channel_id=1, replica_groups=mesh['dp'=8,'mp'=4] {'dp','mp'}, use_global_device_ids=true, to_apply=%region_22.23 | all-reduce | flops 4224 | bytes 33792 | tf_op jit(solution)/shard_map/psum | solution.py:296
  1329.5 73.3 %reduce-scatter.15.cloned.1.call-done = f32[64,768]{1,0:T(8,128)} async-done(((f32[2048,768]{1,0:T(8,128)}), f32[64,768]{1,0:T(8,128)}) %reduce-scatter.15.cloned.1.call-update) | async-done | bytes 196624 | tf_op jit(solution)/shard_map/reduce_scatter | solution.py:295
  (289 shorter events, 170.4 us)
Async XLA Ops:
  7.2 49.3 %copy-start = (bf16[384,2048]{1,0:T(8,128)(2,1)S(1)}, bf16[384,2048]{1,0:T(8,128)(2,1)}, u32[]{:S(2)}) copy-start(bf16[384,2048]{1,0:T(8,128)(2,1)} %param.34) | copy-start | bytes 4718596
  7.2 348.5 %all-reduce.5.cloned.1.call-start = ((), (), s32[]{:S(2)}) async-start(), calls=%async_computation.8 | async-start | bytes 16777216 | tf_op jit(solution)/shard_map/psum | solution.py:173
  7.3 26.9 %copy-start.56 = (s32[6]{0:T(128)}, s32[6]{0:T(128)S(1)}, u32[]{:S(2)}) copy-start(s32[6]{0:T(128)S(1)} %fusion.88) | copy-start | bytes 76
  8.2 16.2 %copy-start.54 = (f32[2048]{0:T(1024)}, f32[2048]{0:T(1024)S(1)}, u32[]{:S(2)}) copy-start(f32[2048]{0:T(1024)S(1)} %convert_element_type.146) | copy-start | bytes 24580
  11.6 27.4 %copy-start.63 = (f32[64]{0:T(128)}, f32[64]{0:T(128)S(1)}, u32[]{:S(2)}) copy-start(f32[64]{0:T(128)S(1)} %convert_element_type.151) | copy-start | bytes 772
  15.1 23.9 %copy-start.10 = (f32[1024,384]{0,1:T(8,128)}, f32[1024,384]{0,1:T(8,128)S(1)}, u32[]{:S(2)}) copy-start(f32[1024,384]{0,1:T(8,128)S(1)} %fusion.103) | copy-start | bytes 4718596
  15.3 23.6 %copy-start.47 = (f32[1024,6]{0,1:T(8,128)}, f32[1024,6]{0,1:T(8,128)S(1)}, u32[]{:S(2)}) copy-start(f32[1024,6]{0,1:T(8,128)S(1)} %add_rsqrt_fusion.1) | copy-start | bytes 73732
  15.3 23.6 %copy-start.58 = (f32[64]{0:T(128)}, f32[64]{0:T(128)S(1)}, u32[]{:S(2)}) copy-start(f32[64]{0:T(128)S(1)} %convert_element_type.153) | copy-start | bytes 772
  37.1 16.6 %copy-start.38 = (bf16[512,6,64]{0,1,2:T(8,128)(2,1)}, bf16[512,6,64]{0,1,2:T(8,128)(2,1)S(1)}, u32[]{:S(2)}) copy-start(bf16[512,6,64]{0,1,2:T(8,128)(2,1)S(1)} %slice.197) | copy-start | bytes 1179652
  62.2 1136.5 %reduce-scatter.19.cloned.1.call-start = ((), (), s32[]{:S(2)}) async-start(), calls=%async_computation.14 | async-start | bytes 5308416 | tf_op jit(solution)/shard_map/reduce_scatter | solution.py:285
  361.4 14.9 %slice-start.5 = ((s8[4718592]{0:T(1024)(128)(4,1)}), s8[524288]{0:T(1024)(128)(4,1)S(1)}, s32[]{:S(2)}) async-start(s8[4718592]{0:T(1024)(128)(4,1)} %bitcast.159), calls=%async_computation.22 | async-start | bytes 1048576
  364.7 31.1 %copy-start.30 = (bf16[1024,2048]{1,0:T(8,128)(2,1)}, bf16[1024,2048]{1,0:T(8,128)(2,1)S(1)}, u32[]{:S(2)}) copy-start(bf16[1024,2048]{1,0:T(8,128)(2,1)S(1)} %multiply_convert_fusion.1) | copy-start | bytes 12582916
  404.6 796.3 %reduce-scatter.21.cloned.1.call-start = ((), (), s32[]{:S(2)}) async-start(), calls=%async_computation.15 | async-start | bytes 5308416 | tf_op jit(solution)/shard_map/reduce_scatter | solution.py:288
  424.0 182.4 %collective-permute-start = (f32[1024,2048]{1,0:T(8,128)}, f32[1024,2048]{1,0:T(8,128)}, u32[]{:S(2)}, u32[]{:S(2)}) collective-permute-start(f32[1024,2048]{1,0:T(8,128)} %convolution_add_fusion), channel_id=1, source_target_pairs={{0,1},{1,0},{2,3},{3,2},{4,5},{5,4},{6,7},{7,6},{8,9},{9,8},{10,11... | collective-permute-start | bytes 25165832 | tf_op jit(solution)/shard_map/ppermute | solution.py:205
  431.4 771.6 %reduce-scatter.23.cloned.1.call-start = ((), (), s32[]{:S(2)}) async-start(), calls=%async_computation.16 | async-start | bytes 5308416 | tf_op jit(solution)/shard_map/reduce_scatter | solution.py:291
  431.4 188.2 %copy-start.28 = (bf16[1024,2048]{1,0:T(8,128)(2,1)S(1)}, bf16[1024,2048]{1,0:T(8,128)(2,1)}, u32[]{:S(2)}) copy-start(bf16[1024,2048]{1,0:T(8,128)(2,1)} %param.39) | copy-start | bytes 12582916
  618.2 429.6 %collective-permute-start.1 = (f32[1024,2048]{1,0:T(8,128)}, f32[1024,2048]{1,0:T(8,128)}, u32[]{:S(2)}, u32[]{:S(2)}) collective-permute-start(f32[1024,2048]{1,0:T(8,128)} %add.217), channel_id=1, source_target_pairs={{0,2},{1,3},{2,0},{3,1},{4,6},{5,7},{6,4},{7,5},{8,10},{9,11},{10,... | collective-permute-start | bytes 25165832 | tf_op jit(solution)/shard_map/ppermute | solution.py:205
  628.2 577.1 %reduce-scatter.9.cloned.1.call-start = ((), (), s32[]{:S(2)}) async-start(), calls=%async_computation.9 | async-start | bytes 5242880 | tf_op jit(solution)/shard_map/reduce_scatter | solution.py:183
  628.9 442.0 %copy-start.52 = (f32[6,512]{1,0:T(8,128)}, f32[6,512]{1,0:T(8,128)S(1)}, u32[]{:S(2)}) copy-start(f32[6,512]{1,0:T(8,128)S(1)} %log_add_fusion.1) | copy-start | bytes 36868
  638.7 570.7 %reduce-scatter.13.cloned.1.call-start = ((), (), s32[]{:S(2)}) async-start(), calls=%async_computation.11 | async-start | bytes 1769472 | tf_op jit(solution)/shard_map/reduce_scatter | solution.py:279
  638.7 421.8 %copy-start.29 = (bf16[1024,2048]{1,0:T(8,128)(2,1)S(1)}, bf16[1024,2048]{1,0:T(8,128)(2,1)}, u32[]{:S(2)}) copy-start(bf16[1024,2048]{1,0:T(8,128)(2,1)} %param.39) | copy-start | bytes 12582916
  1122.3 88.8 %reduce-scatter.17.cloned.1.call-start = ((), (), s32[]{:S(2)}) async-start(), calls=%async_computation.13 | async-start | bytes 1769472 | tf_op jit(solution)/shard_map/reduce_scatter | solution.py:282
  1128.8 152.4 %reduce-scatter.11.cloned.1.call-start = ((), (), s32[]{:S(2)}) async-start(), calls=%async_computation.10 | async-start | bytes 5242880 | tf_op jit(solution)/shard_map/reduce_scatter | solution.py:273
  1142.9 260.0 %reduce-scatter.15.cloned.1.call-start = ((), (), s32[]{:S(2)}) async-start(), calls=%async_computation.12 | async-start | bytes 6488064 | tf_op jit(solution)/shard_map/reduce_scatter | solution.py:295
  (67 other events, 312.6 us)
Sparse Core Ops, SparseCore 0:
  62.3 293.3 all-reduce.4
  404.7 52.7 reduce-scatter.18
  461.0 53.7 reduce-scatter.20
  628.3 52.7 reduce-scatter.22
  683.2 204.9 reduce-scatter.8
  1122.5 37.9 reduce-scatter.12
  1163.7 38.2 reduce-scatter.16
  1204.3 76.7 reduce-scatter.10
  1287.4 115.4 reduce-scatter.14
